TPU v7x, 32 devices: a whole 2x2x4 slice. The times are simulated.
32 devices in a mesh: dp: 16 (over z, y, core), expert: 2 (over x).
Axes of the slice: x: 2, y: 2, z: 4, core: 2. Of those that a mesh axis runs over, the one named last changes fastest.
Arguments:
- tokens: bfloat16 [256, 6144], P('dp', 'expert'), may hold values from -6 to 6
- expert_ids: int32 [256, 2], P('dp'), may hold values from 0 to 7, all different within a row; in each aligned block of 16 rows (0 to 15, 16 to 31, ...) at most 8 rows name the same one
- gate_probs: float32 [256, 2], P('dp'), may hold values from 0.1 to 1
- w_gate: bfloat16 [8, 6144, 8192], P('expert', None, 'dp'), may hold values from -0.078125 to 0.078125
- w_up: bfloat16 [8, 6144, 8192], P('expert', None, 'dp'), may hold values from -0.078125 to 0.078125
- w_down_t: bfloat16 [8, 6144, 8192], P('expert', 'dp'), may hold values from -0.0625 to 0.0625
Outputs:
- mixed: bfloat16 [256, 6144], P('dp', 'expert')
Inputs may be any that keep to these rules, and one draw needn't show every extreme that they name: `expert_ids`: each row names 2 different experts. Among the 16 rows of one index of dp no expert is named more than 8 times, a bound that some block reaches.
All inputs are finite; a program needn't handle non-finite values.
Results may differ from a plain program's by a relative error of at most 0.0057.
Values may be sent and summed in bfloat16 or wider, within the bound.
A program may use at most 128 MiB of HBM per device.

v0:
```python
import jax
import jax.numpy as jnp
from jax import lax
from jax.sharding import PartitionSpec as P


def assignments(expert_ids, experts, capacity):
    flat = expert_ids.reshape(-1)
    onehot = (flat[:, None] == jnp.arange(experts, dtype=jnp.int32)[None, :]).astype(jnp.int32)
    earlier = jnp.cumsum(onehot, axis=0) - onehot
    position = jnp.sum(earlier * onehot, axis=1).reshape(expert_ids.shape)
    expert_hit = (
        expert_ids[:, :, None] == jnp.arange(experts, dtype=jnp.int32)[None, None, :]
    ).astype(jnp.float32)
    slot_hit = (
        position[:, :, None] == jnp.arange(capacity, dtype=jnp.int32)[None, None, :]
    ).astype(jnp.float32)
    return (expert_hit, slot_hit)


def per_device(tokens, expert_ids, gate_probs, w_gate, w_up, w_down_t):
    local_experts = w_gate.shape[0]
    expert_count = lax.axis_size("expert")
    dp_count = lax.axis_size("dp")
    experts = local_experts * expert_count
    capacity = tokens.shape[0] // 2
    expert_hit, slot_hit = assignments(expert_ids, experts, capacity)
    dispatch_map = jnp.einsum("tke,tkc->ect", expert_hit, slot_hit).astype(jnp.bfloat16)
    combine_map = jnp.einsum(
        "tk,tke,tkc->tec", gate_probs, expert_hit, slot_hit, precision=lax.Precision.HIGHEST
    )
    slots = jnp.einsum(
        "ect,td->ecd", dispatch_map, tokens, preferred_element_type=jnp.float32
    ).astype(jnp.bfloat16)
    arrived = lax.all_to_all(slots, "expert", split_axis=0, concat_axis=2, tiled=True)
    piece = lax.all_gather(arrived, "dp", axis=1, tiled=True)
    gate = jnp.einsum("erd,edf->erf", piece, w_gate, preferred_element_type=jnp.float32)
    up = jnp.einsum("erd,edf->erf", piece, w_up, preferred_element_type=jnp.float32)
    hidden = (jax.nn.silu(gate) * up).astype(jnp.bfloat16)
    partial_out = jnp.einsum(
        "erf,edf->erd",
        lax.all_gather(hidden, "dp", axis=2, tiled=True),
        w_down_t,
        preferred_element_type=jnp.float32,
    )
    results = partial_out.astype(jnp.bfloat16).reshape(
        local_experts, dp_count, capacity, w_down_t.shape[1]
    )
    results = lax.all_to_all(results, "dp", split_axis=1, concat_axis=3, tiled=True)
    results = results.reshape(local_experts, capacity, results.shape[3])
    slice_width = tokens.shape[1]
    outgoing = results.reshape(local_experts, capacity, expert_count, slice_width)
    returned = lax.all_to_all(outgoing, "expert", split_axis=2, concat_axis=0, tiled=True)
    returned = returned.reshape(experts, capacity, slice_width)
    mixed = jnp.einsum(
        "tec,ecd->td", combine_map, returned.astype(jnp.float32), precision=lax.Precision.HIGHEST
    )
    return mixed.astype(jnp.bfloat16)


def solution(mesh):
    placed = (
        P("dp", "expert"),
        P("dp", None),
        P("dp", None),
        P("expert", None, "dp"),
        P("expert", None, "dp"),
        P("expert", "dp", None),
    )
    return jax.shard_map(
        per_device, mesh=mesh, in_specs=placed, out_specs=P("dp", "expert"), check_vma=False
    )
```

profile of v0, /device:TPU:0, one launch (start us, length us, event | category | flops | bytes accessed | tf_op | source)
XLA Modules:
  0.0 233.5 jit_solution(2106220213072693453)
XLA Ops:
  6.5 0.0 copy-start
  6.5 0.0 all-gather.3.cloned.1.call-start
  6.5 0.8 copy.17
  7.3 0.1 eq.46
  7.4 0.1 fusion.7
  7.5 0.1 reduce_window_sum.11
  7.5 0.2 select_reduce_fusion
  7.7 0.1 eq.50
  7.8 0.3 fusion.3
  8.1 0.1 copy.20
  8.2 0.0 copy-done
  8.2 0.2 convolution_convert_fusion
  8.5 10.6 %all_to_all.48 = bf16[8,8,3072]{2,1,0:T(8,128)(2,1)S(1)} all-to-all(bf16[8,8,3072]{2,1,0:T(8,128)(2,1)S(1)} %convolution_convert_fusion), channel_id=1, replica_groups=mesh['dp'=16,'expert'=2] {'expert'}, dimensions={0} | all-to-all | bytes 786432 | tf_op jit(solution)/shard_map/all_to_all | solution.py:35
  19.1 0.8 copy.21
  19.9 0.0 all-gather.3.cloned.1.call-update
  19.9 0.0 all-gather.5.cloned.1.call-start
  19.9 62.0 %all-gather.3.cloned.1.call-done = bf16[4,128,6144]{2,1,0:T(8,128)(2,1)} async-done(((bf16[4,8,6144]{2,1,0:T(8,128)(2,1)}), bf16[4,128,6144]{2,1,0:T(8,128)(2,1)}) %all-gather.3.cloned.1.call-update) | async-done | bytes 6291472 | tf_op jit(solution)/shard_map/all_gather | solution.py:36
  81.9 0.0 copy-start.2
  81.9 11.9 %fusion.16 = f32[4,128,512]{2,1,0:T(8,128)S(1)} fusion(bf16[4,128,6144]{2,1,0:T(8,128)(2,1)} %all-gather.3.cloned.1.call-done, bf16[4,6144,512]{2,1,0:T(8,128)(2,1)} %param.9), kind=kOutput, calls=%fused_computation.25 | convolution fusion | flops 3221225472 | bytes 32505856 | tf_op jit(solution)/shard_map/erd,edf->erf/dot_general | solution.py:37
  93.8 0.0 copy-done.2
  93.9 0.0 copy-start.1
  93.9 12.6 %fusion.1 = bf16[4,128,512]{2,1,0:T(8,128)(2,1)} fusion(bf16[4,128,6144]{2,1,0:T(8,128)(2,1)S(1)} %copy-done.2, bf16[4,6144,512]{2,1,0:T(8,128)(2,1)} %param.10, f32[4,128,512]{2,1,0:T(8,128)S(1)} %fusion.16), kind=kOutput, calls=%fused_computation.4 | convolution fusion | flops 3222798336 | bytes 33030144 | tf_op jit(solution)/shard_map/erd,edf->erf/dot_general | solution.py:38
  106.4 0.0 copy-start.3
  106.4 0.0 all-gather.5.cloned.1.call-update
  106.5 76.5 %all-gather.5.cloned.1.call-done = bf16[4,128,8192]{2,1,0:T(8,128)(2,1)} async-done(((bf16[4,128,512]{2,1,0:T(8,128)(2,1)}), bf16[4,128,8192]{2,1,0:T(8,128)(2,1)}) %all-gather.5.cloned.1.call-update) | async-done | bytes 8388624 | tf_op jit(solution)/shard_map/all_gather | solution.py:42
  183.0 14.5 %fusion.2 = bf16[4,16,8,384]{3,2,1,0:T(8,128)(2,1)S(1)} fusion(bf16[4,128,8192]{2,1,0:T(8,128)(2,1)} %all-gather.5.cloned.1.call-done, bf16[4,384,8192]{2,1,0:T(8,128)(2,1)} %param.11), kind=kOutput, calls=%fused_computation.6 | convolution fusion | flops 3221422080 | bytes 33947648 | tf_op jit(solution)/shard_map/erf,edf->erd/dot_general | solution.py:40
  197.5 0.8 copy.22
  198.3 3.6 %all-to-all-start.1 = ((bf16[4,16,8,384]{3,2,0,1:T(8,128)(2,1)}), bf16[4,16,8,384]{3,2,0,1:T(8,128)(2,1)S(1)}, u32[]{:S(2)}, u32[]{:S(2)}) async-start(bf16[4,16,8,384]{3,2,0,1:T(8,128)(2,1)} %copy.22), calls=%async_computation.1 | async-start | bytes 786432 | tf_op jit(solution)/shard_map/all_to_all | solution.py:49
  201.8 0.0 copy-done.3
  201.8 0.1 copy.18
  201.9 12.0 %all-to-all-done.1 = bf16[4,16,8,384]{3,2,0,1:T(8,128)(2,1)S(1)} async-done(((bf16[4,16,8,384]{3,2,0,1:T(8,128)(2,1)}), bf16[4,16,8,384]{3,2,0,1:T(8,128)(2,1)S(1)}, u32[]{:S(2)}, u32[]{:S(2)}) %all-to-all-start.1) | async-done | bytes 393248 | tf_op jit(solution)/shard_map/all_to_all | solution.py:49
  213.9 0.1 copy.23
  214.1 0.1 reshape_reshape.3
  214.2 0.8 copy.24
  215.0 3.5 %all-to-all-start.2 = ((bf16[4,8,2,3072]{3,1,0,2:T(8,128)(2,1)}), bf16[4,8,2,3072]{3,1,0,2:T(8,128)(2,1)S(1)}, u32[]{:S(2)}, u32[]{:S(2)}) async-start(bf16[4,8,2,3072]{3,1,0,2:T(8,128)(2,1)} %copy.24), calls=%async_computation.2 | async-start | bytes 786432 | tf_op jit(solution)/shard_map/all_to_all | solution.py:53
  218.5 0.4 fusion.6
  218.9 0.1 copy.26
  219.0 6.6 %all-to-all-done.2 = bf16[4,8,2,3072]{3,1,0,2:T(8,128)(2,1)S(1)} async-done(((bf16[4,8,2,3072]{3,1,0,2:T(8,128)(2,1)}), bf16[4,8,2,3072]{3,1,0,2:T(8,128)(2,1)S(1)}, u32[]{:S(2)}, u32[]{:S(2)}) %all-to-all-start.2) | async-done | bytes 393248 | tf_op jit(solution)/shard_map/all_to_all | solution.py:53
  225.6 1.1 fusion
  226.7 0.0 copy-done.1
Async XLA Ops:
  6.5 1.7 copy-start
  6.5 75.4 %all-gather.3.cloned.1.call-start = ((), (), s32[]{:S(2)}) async-start(), calls=%async_computation.3 | async-start | bytes 6684672 | tf_op jit(solution)/shard_map/all_gather | solution.py:36
  19.9 163.1 %all-gather.5.cloned.1.call-start = ((), (), s32[]{:S(2)}) async-start(), calls=%async_computation.4 | async-start | bytes 8912896 | tf_op jit(solution)/shard_map/all_gather | solution.py:42
  81.9 11.9 %copy-start.2 = (bf16[4,128,6144]{2,1,0:T(8,128)(2,1)S(1)}, bf16[4,128,6144]{2,1,0:T(8,128)(2,1)}, u32[]{:S(2)}) copy-start(bf16[4,128,6144]{2,1,0:T(8,128)(2,1)} %all-gather.3.cloned.1.call-done) | copy-start | bytes 18874372
  93.9 132.8 %copy-start.1 = (bf16[16,3072]{1,0:T(8,128)(2,1)S(1)}, bf16[16,3072]{1,0:T(8,128)(2,1)}, u32[]{:S(2)}) copy-start(bf16[16,3072]{1,0:T(8,128)(2,1)} %param.6) | copy-start | bytes 294916
  106.4 95.4 %copy-start.3 = (f32[16,2]{0,1:T(2,128)S(1)}, f32[16,2]{0,1:T(2,128)}, u32[]{:S(2)}) copy-start(f32[16,2]{0,1:T(2,128)} %param.8) | copy-start | bytes 388
  198.3 15.7 %all-to-all-start.1 = ((bf16[4,16,8,384]{3,2,0,1:T(8,128)(2,1)}), bf16[4,16,8,384]{3,2,0,1:T(8,128)(2,1)S(1)}, u32[]{:S(2)}, u32[]{:S(2)}) async-start(bf16[4,16,8,384]{3,2,0,1:T(8,128)(2,1)} %copy.22), calls=%async_computation.1 | async-start | bytes 786432 | tf_op jit(solution)/shard_map/all_to_all | solution.py:49
  215.0 10.6 %all-to-all-start.2 = ((bf16[4,8,2,3072]{3,1,0,2:T(8,128)(2,1)}), bf16[4,8,2,3072]{3,1,0,2:T(8,128)(2,1)S(1)}, u32[]{:S(2)}, u32[]{:S(2)}) async-start(bf16[4,8,2,3072]{3,1,0,2:T(8,128)(2,1)} %copy.24), calls=%async_computation.2 | async-start | bytes 786432 | tf_op jit(solution)/shard_map/all_to_all | solution.py:53
Sparse Core Ops, SparseCore 0:
  20.0 61.8 all-gather.2
  106.6 76.3 all-gather.4
where the time goes:
time: 234 us
  waiting for transfers between devices  157 us (67%)
  matrix products  41 us (18%)
  between operations  13.5 us (6%)
  blocking collectives  10.6 us (5%)
  starting transfers between devices  7.06 us (3%)
  local copies, waits for them, and re-layouts  3.83 us (2%)
    all_gather x1, waiting for transfers between devices, per_device(): lax.all_gather(hidden, 'dp', axis=2, tiled=True)  76.5 us
    all_gather x1, waiting for transfers between devices, per_device(): piece = lax.all_gather(arrived, 'dp', axis=1, tiled=True)  62 us
    dot_general x1, matrix products, per_device(): jnp.einsum('erf,edf->erd', lax.all_gather(hidden, 'dp', axis=2, tiled=Tru...  14.5 us
    dot_general x1, matrix products, per_device(): jnp.einsum('erd,edf->erf', piece, w_up, preferred_element_type=jnp.float32)  12.6 us
    all_to_all x1, waiting for transfers between devices, per_device(): lax.all_to_all(results, 'dp', split_axis=1, concat_axis=3, tiled=True)  12 us
    dot_general x1, matrix products, per_device(): jnp.einsum('erd,edf->erf', piece, w_gate, preferred_element_type=jnp.floa...  11.9 us
    all_to_all x1, blocking collectives, per_device(): lax.all_to_all(slots, 'expert', split_axis=0, concat_axis=2, tiled=True)  10.6 us
    all_to_all x1, waiting for transfers between devices, per_device(): lax.all_to_all(outgoing, 'expert', split_axis=2, concat_axis=0, tiled=True)  6.61 us
  transfers between devices with their start and end apart: 4, of which 4 were waited for; matrix products, arithmetic and copies ran while one was open for 0% of the time, Pallas kernels for 0%

commit v1 on v0

--- a/solution.py
+++ b/solution.py
@@ -2,6 +2,18 @@
 import jax.numpy as jnp
 from jax import lax
 from jax.sharding import PartitionSpec as P
+
+
+def summed_around(shard, axis, dim, term):
+    size, index, extent = (lax.axis_size(axis), lax.axis_index(axis), shard.shape[dim])
+    right = [(i, (i + 1) % size) for i in range(size)]
+    held, total = (shard, None)
+    for lap in range(size):
+        arriving = lax.ppermute(held, axis, right) if lap < size - 1 else None
+        update = term(held, (index - lap) % size * extent)
+        total = update if total is None else total + update
+        held = arriving
+    return total
 
 
 def assignments(expert_ids, experts, capacity):
@@ -37,11 +49,16 @@
     gate = jnp.einsum("erd,edf->erf", piece, w_gate, preferred_element_type=jnp.float32)
     up = jnp.einsum("erd,edf->erf", piece, w_up, preferred_element_type=jnp.float32)
     hidden = (jax.nn.silu(gate) * up).astype(jnp.bfloat16)
-    partial_out = jnp.einsum(
-        "erf,edf->erd",
-        lax.all_gather(hidden, "dp", axis=2, tiled=True),
-        w_down_t,
-        preferred_element_type=jnp.float32,
+    partial_out = summed_around(
+        hidden,
+        "dp",
+        2,
+        lambda own_block, start: jnp.einsum(
+            "erf,edf->erd",
+            own_block,
+            lax.dynamic_slice_in_dim(w_down_t, start, own_block.shape[2], axis=2),
+            preferred_element_type=jnp.float32,
+        ),
     )
     results = partial_out.astype(jnp.bfloat16).reshape(
         local_experts, dp_count, capacity, w_down_t.shape[1]

time: 234 us -> 314 us (1.34)
  waiting for transfers between devices: 157 us -> 218 us
  matrix products: 41 us -> 58.7 us
    ppermute x0 -> x15, waiting for transfers between devices: none -> 137 us  [summed_around(): arriving = lax.ppermute(held, axis, right) if lap < size - 1 else None]
    all_gather x1 -> x0, waiting for transfers between devices: 76.5 us -> none  [per_device(): lax.all_gather(hidden, 'dp', axis=2, tiled=True)]
    dot_general x1 -> x16, matrix products: 14.5 us -> 33 us  [per_device(): jnp.einsum('erf,edf->erd', own_block, lax.dynamic_slice_in_dim(w_down_t,...]
  transfers between devices with their start and end apart: 4 -> 18, of which waited for: 4 -> 18; matrix products, arithmetic and copies ran while one was open for 0% -> 10% of each run, Pallas kernels for 0% -> 0%
where the time goes in v1:
time: 314 us
  waiting for transfers between devices  218 us (69%)
  matrix products  58.7 us (19%)
  between operations  13.6 us (4%)
  blocking collectives  10.6 us (3%)
  starting transfers between devices  7.36 us (2%)
  local copies, waits for them, and re-layouts  5.46 us (2%)
    ppermute x15, waiting for transfers between devices, summed_around(): arriving = lax.ppermute(held, axis, right) if lap < size - 1 else None  137 us
    all_gather x1, waiting for transfers between devices, per_device(): piece = lax.all_gather(arrived, 'dp', axis=1, tiled=True)  62 us
    dot_general x16, matrix products, per_device(): jnp.einsum('erf,edf->erd', own_block, lax.dynamic_slice_in_dim(w_down_t,...  33 us
    all_to_all x1, waiting for transfers between devices, per_device(): lax.all_to_all(results, 'dp', split_axis=1, concat_axis=3, tiled=True)  12 us
    dot_general x1, matrix products, per_device(): jnp.einsum('erd,edf->erf', piece, w_gate, preferred_element_type=jnp.floa...  11.9 us
    dot_general x1, matrix products, per_device(): jnp.einsum('erd,edf->erf', piece, w_up, preferred_element_type=jnp.float32)  11.7 us
    all_to_all x1, blocking collectives, per_device(): lax.all_to_all(slots, 'expert', split_axis=0, concat_axis=2, tiled=True)  10.6 us
    all_to_all x1, waiting for transfers between devices, per_device(): lax.all_to_all(outgoing, 'expert', split_axis=2, concat_axis=0, tiled=True)  6.61 us
  transfers between devices with their start and end apart: 18, of which 18 were waited for; matrix products, arithmetic and copies ran while one was open for 10% of the time, Pallas kernels for 0%

profile of v1, /device:TPU:0, one launch (start us, length us, event | category | flops | bytes accessed | tf_op | source)
XLA Modules:
  0.0 313.6 jit_solution(13014385433815353440)
XLA Ops:
  6.5 0.8 copy.17
  7.3 0.1 eq.63
  7.4 0.1 fusion.89
  7.5 0.1 reduce_window_sum.11
  7.5 0.2 select_reduce_fusion
  7.7 0.1 eq.67
  7.8 0.3 fusion.85
  8.1 0.1 copy.20
  8.2 0.2 convolution_convert_fusion
  8.5 10.6 %all_to_all.48 = bf16[8,8,3072]{2,1,0:T(8,128)(2,1)S(1)} all-to-all(bf16[8,8,3072]{2,1,0:T(8,128)(2,1)S(1)} %convolution_convert_fusion), channel_id=1, replica_groups=mesh['dp'=16,'expert'=2] {'expert'}, dimensions={0} | all-to-all | bytes 786432 | tf_op jit(solution)/shard_map/all_to_all | solution.py:47
  19.1 0.8 copy.21
  19.9 0.0 all-gather.2.cloned.1.call-update
  19.9 62.0 %all-gather.2.cloned.1.call-done = bf16[4,128,6144]{2,1,0:T(8,128)(2,1)} async-done(((bf16[4,8,6144]{2,1,0:T(8,128)(2,1)}), bf16[4,128,6144]{2,1,0:T(8,128)(2,1)}) %all-gather.2.cloned.1.call-update) | async-done | bytes 6291472 | tf_op jit(solution)/shard_map/all_gather | solution.py:48
  81.9 11.9 %fusion.114 = f32[4,128,512]{2,1,0:T(8,128)S(1)} fusion(bf16[4,128,6144]{2,1,0:T(8,128)(2,1)} %all-gather.2.cloned.1.call-done, bf16[4,6144,512]{2,1,0:T(8,128)(2,1)} %param.9), kind=kOutput, calls=%fused_computation.88 | convolution fusion | flops 3221225472 | bytes 32505856 | tf_op jit(solution)/shard_map/erd,edf->erf/dot_general | solution.py:49
  93.9 11.7 %fusion.78 = bf16[4,128,512]{2,1,0:T(8,128)(2,1)S(1)} fusion(bf16[4,128,6144]{2,1,0:T(8,128)(2,1)S(1)} %copy-done.2, bf16[4,6144,512]{2,1,0:T(8,128)(2,1)} %param.10, f32[4,128,512]{2,1,0:T(8,128)S(1)} %fusion.114), kind=kOutput, calls=%fused_computation.51 | convolution fusion | flops 3222798336 | bytes 33030144 | tf_op jit(solution)/shard_map/erd,edf->erf/dot_general | solution.py:50
  105.6 0.3 collective-permute-start
  105.9 11.1 %collective-permute-done = bf16[4,128,512]{2,1,0:T(8,128)(2,1)S(1)} collective-permute-done((bf16[4,128,512]{2,1,0:T(8,128)(2,1)S(1)}, bf16[4,128,512]{2,1,0:T(8,128)(2,1)S(1)}, u32[]{:S(2)}, u32[]{:S(2)}) %collective-permute-start) | collective-permute-done | bytes 524320 | tf_op jit(solution)/shard_map/ppermute | solution.py:12
  116.9 11.3 %collective-permute-done.1 = bf16[4,128,512]{2,1,0:T(8,128)(2,1)S(1)} collective-permute-done((bf16[4,128,512]{2,1,0:T(8,128)(2,1)S(1)}, bf16[4,128,512]{2,1,0:T(8,128)(2,1)S(1)}, u32[]{:S(2)}, u32[]{:S(2)}) %collective-permute-start.1) | collective-permute-done | bytes 524320 | tf_op jit(solution)/shard_map/ppermute | solution.py:12
  128.2 0.0 collective-permute-start.2
  128.2 0.8 copy-done.5
  129.0 10.5 %collective-permute-done.2 = bf16[4,128,512]{2,1,0:T(8,128)(2,1)S(1)} collective-permute-done((bf16[4,128,512]{2,1,0:T(8,128)(2,1)S(1)}, bf16[4,128,512]{2,1,0:T(8,128)(2,1)S(1)}, u32[]{:S(2)}, u32[]{:S(2)}) %collective-permute-start.2) | collective-permute-done | bytes 524320 | tf_op jit(solution)/shard_map/ppermute | solution.py:12
  139.5 11.3 %collective-permute-done.3 = bf16[4,128,512]{2,1,0:T(8,128)(2,1)S(1)} collective-permute-done((bf16[4,128,512]{2,1,0:T(8,128)(2,1)S(1)}, bf16[4,128,512]{2,1,0:T(8,128)(2,1)S(1)}, u32[]{:S(2)}, u32[]{:S(2)}) %collective-permute-start.3) | collective-permute-done | bytes 524320 | tf_op jit(solution)/shard_map/ppermute | solution.py:12
  150.8 0.8 copy-done.4
  151.6 10.5 %collective-permute-done.4 = bf16[4,128,512]{2,1,0:T(8,128)(2,1)S(1)} collective-permute-done((bf16[4,128,512]{2,1,0:T(8,128)(2,1)S(1)}, bf16[4,128,512]{2,1,0:T(8,128)(2,1)S(1)}, u32[]{:S(2)}, u32[]{:S(2)}) %collective-permute-start.4) | collective-permute-done | bytes 524320 | tf_op jit(solution)/shard_map/ppermute | solution.py:12
  162.1 11.3 %collective-permute-done.5 = bf16[4,128,512]{2,1,0:T(8,128)(2,1)S(1)} collective-permute-done((bf16[4,128,512]{2,1,0:T(8,128)(2,1)S(1)}, bf16[4,128,512]{2,1,0:T(8,128)(2,1)S(1)}, u32[]{:S(2)}, u32[]{:S(2)}) %collective-permute-start.5) | collective-permute-done | bytes 524320 | tf_op jit(solution)/shard_map/ppermute | solution.py:12
  173.5 11.3 %collective-permute-done.6 = bf16[4,128,512]{2,1,0:T(8,128)(2,1)S(1)} collective-permute-done((bf16[4,128,512]{2,1,0:T(8,128)(2,1)S(1)}, bf16[4,128,512]{2,1,0:T(8,128)(2,1)S(1)}, u32[]{:S(2)}, u32[]{:S(2)}) %collective-permute-start.6) | collective-permute-done | bytes 524320 | tf_op jit(solution)/shard_map/ppermute | solution.py:12
  184.8 2.0 fusion.31
  186.8 9.4 %collective-permute-done.7 = bf16[4,128,512]{2,1,0:T(8,128)(2,1)} collective-permute-done((bf16[4,128,512]{2,1,0:T(8,128)(2,1)S(1)}, bf16[4,128,512]{2,1,0:T(8,128)(2,1)}, u32[]{:S(2)}, u32[]{:S(2)}) %collective-permute-start.7) | collective-permute-done | bytes 524320 | tf_op jit(solution)/shard_map/ppermute | solution.py:12
  196.2 2.0 fusion.33
  198.2 2.2 fusion.36
  200.4 0.0 copy-start.6
  200.4 7.3 %collective-permute-done.8 = bf16[4,128,512]{2,1,0:T(8,128)(2,1)S(1)} collective-permute-done((bf16[4,128,512]{2,1,0:T(8,128)(2,1)}, bf16[4,128,512]{2,1,0:T(8,128)(2,1)S(1)}, u32[]{:S(2)}, u32[]{:S(2)}) %collective-permute-start.8) | collective-permute-done | bytes 524320 | tf_op jit(solution)/shard_map/ppermute | solution.py:12
  207.7 2.1 fusion.39
  209.7 2.2 fusion.42
  211.9 7.0 %collective-permute-done.9 = bf16[4,128,512]{2,1,0:T(8,128)(2,1)S(1)} collective-permute-done((bf16[4,128,512]{2,1,0:T(8,128)(2,1)S(1)}, bf16[4,128,512]{2,1,0:T(8,128)(2,1)S(1)}, u32[]{:S(2)}, u32[]{:S(2)}) %collective-permute-start.9) | collective-permute-done | bytes 524320 | tf_op jit(solution)/shard_map/ppermute | solution.py:12
  219.0 2.0 fusion.45
  221.0 2.2 fusion.48
  223.2 7.1 %collective-permute-done.10 = bf16[4,128,512]{2,1,0:T(8,128)(2,1)S(1)} collective-permute-done((bf16[4,128,512]{2,1,0:T(8,128)(2,1)S(1)}, bf16[4,128,512]{2,1,0:T(8,128)(2,1)S(1)}, u32[]{:S(2)}, u32[]{:S(2)}) %collective-permute-start.10) | collective-permute-done | bytes 524320 | tf_op jit(solution)/shard_map/ppermute | solution.py:12
  230.3 2.0 fusion.51
  232.3 2.2 fusion.54
  234.5 7.1 %collective-permute-done.11 = bf16[4,128,512]{2,1,0:T(8,128)(2,1)S(1)} collective-permute-done((bf16[4,128,512]{2,1,0:T(8,128)(2,1)S(1)}, bf16[4,128,512]{2,1,0:T(8,128)(2,1)S(1)}, u32[]{:S(2)}, u32[]{:S(2)}) %collective-permute-start.11) | collective-permute-done | bytes 524320 | tf_op jit(solution)/shard_map/ppermute | solution.py:12
  241.6 0.0 collective-permute-start.12
  241.6 2.0 fusion.57
  243.6 2.0 fusion.60
  245.7 7.2 %collective-permute-done.12 = bf16[4,128,512]{2,1,0:T(8,128)(2,1)S(1)} collective-permute-done((bf16[4,128,512]{2,1,0:T(8,128)(2,1)S(1)}, bf16[4,128,512]{2,1,0:T(8,128)(2,1)S(1)}, u32[]{:S(2)}, u32[]{:S(2)}) %collective-permute-start.12) | collective-permute-done | bytes 524320 | tf_op jit(solution)/shard_map/ppermute | solution.py:12
  252.9 2.0 fusion.63
  254.9 2.0 fusion.66
  257.0 7.2 %collective-permute-done.13 = bf16[4,128,512]{2,1,0:T(8,128)(2,1)S(1)} collective-permute-done((bf16[4,128,512]{2,1,0:T(8,128)(2,1)S(1)}, bf16[4,128,512]{2,1,0:T(8,128)(2,1)S(1)}, u32[]{:S(2)}, u32[]{:S(2)}) %collective-permute-start.13) | collective-permute-done | bytes 524320 | tf_op jit(solution)/shard_map/ppermute | solution.py:12
  264.2 2.0 fusion.69
  266.2 2.0 fusion.72
  268.3 7.2 %collective-permute-done.14 = bf16[4,128,512]{2,1,0:T(8,128)(2,1)S(1)} collective-permute-done((bf16[4,128,512]{2,1,0:T(8,128)(2,1)S(1)}, bf16[4,128,512]{2,1,0:T(8,128)(2,1)S(1)}, u32[]{:S(2)}, u32[]{:S(2)}) %collective-permute-start.14) | collective-permute-done | bytes 524320 | tf_op jit(solution)/shard_map/ppermute | solution.py:12
  275.5 2.0 fusion.82
  277.5 0.8 copy.22
  278.3 3.6 %all-to-all-start.1 = ((bf16[4,16,8,384]{3,2,0,1:T(8,128)(2,1)}), bf16[4,16,8,384]{3,2,0,1:T(8,128)(2,1)S(1)}, u32[]{:S(2)}, u32[]{:S(2)}) async-start(bf16[4,16,8,384]{3,2,0,1:T(8,128)(2,1)} %copy.22), calls=%async_computation.1 | async-start | bytes 786432 | tf_op jit(solution)/shard_map/all_to_all | solution.py:66
  281.9 0.1 copy.18
  282.0 12.0 %all-to-all-done.1 = bf16[4,16,8,384]{3,2,0,1:T(8,128)(2,1)S(1)} async-done(((bf16[4,16,8,384]{3,2,0,1:T(8,128)(2,1)}), bf16[4,16,8,384]{3,2,0,1:T(8,128)(2,1)S(1)}, u32[]{:S(2)}, u32[]{:S(2)}) %all-to-all-start.1) | async-done | bytes 393248 | tf_op jit(solution)/shard_map/all_to_all | solution.py:66
  294.0 0.1 copy.23
  294.1 0.1 reshape_reshape.3
  294.2 0.8 copy.24
  295.0 3.5 %all-to-all-start.2 = ((bf16[4,8,2,3072]{3,1,0,2:T(8,128)(2,1)}), bf16[4,8,2,3072]{3,1,0,2:T(8,128)(2,1)S(1)}, u32[]{:S(2)}, u32[]{:S(2)}) async-start(bf16[4,8,2,3072]{3,1,0,2:T(8,128)(2,1)} %copy.24), calls=%async_computation.2 | async-start | bytes 786432 | tf_op jit(solution)/shard_map/all_to_all | solution.py:70
  298.5 0.4 fusion.88
  298.9 0.1 copy.26
  299.0 6.6 %all-to-all-done.2 = bf16[4,8,2,3072]{3,1,0,2:T(8,128)(2,1)S(1)} async-done(((bf16[4,8,2,3072]{3,1,0,2:T(8,128)(2,1)}), bf16[4,8,2,3072]{3,1,0,2:T(8,128)(2,1)S(1)}, u32[]{:S(2)}, u32[]{:S(2)}) %all-to-all-start.2) | async-done | bytes 393248 | tf_op jit(solution)/shard_map/all_to_all | solution.py:70
  305.6 1.1 fusion
  (24 shorter events, 0.1 us)
Async XLA Ops:
  6.5 1.7 copy-start
  6.5 75.4 %all-gather.2.cloned.1.call-start = ((), (), s32[]{:S(2)}) async-start(), calls=%async_computation.3 | async-start | bytes 6684672 | tf_op jit(solution)/shard_map/all_gather | solution.py:48
  81.9 11.9 %copy-start.2 = (bf16[4,128,6144]{2,1,0:T(8,128)(2,1)S(1)}, bf16[4,128,6144]{2,1,0:T(8,128)(2,1)}, u32[]{:S(2)}) copy-start(bf16[4,128,6144]{2,1,0:T(8,128)(2,1)} %all-gather.2.cloned.1.call-done) | copy-start | bytes 18874372
  105.6 11.4 %collective-permute-start = (bf16[4,128,512]{2,1,0:T(8,128)(2,1)S(1)}, bf16[4,128,512]{2,1,0:T(8,128)(2,1)S(1)}, u32[]{:S(2)}, u32[]{:S(2)}) collective-permute-start(bf16[4,128,512]{2,1,0:T(8,128)(2,1)S(1)} %fusion.78), channel_id=1, source_target_pairs={{0,2},{2,4},{4,6},{6,8},{8,10},{10,12},{12,14},{14,16},{16,18},{18... | collective-permute-start | bytes 1572872 | tf_op jit(solution)/shard_map/ppermute | solution.py:12
  116.9 11.3 %collective-permute-start.1 = (bf16[4,128,512]{2,1,0:T(8,128)(2,1)S(1)}, bf16[4,128,512]{2,1,0:T(8,128)(2,1)S(1)}, u32[]{:S(2)}, u32[]{:S(2)}) collective-permute-start(bf16[4,128,512]{2,1,0:T(8,128)(2,1)S(1)} %collective-permute-done), channel_id=1, source_target_pairs={{0,2},{2,4},{4,6},{6,8},{8,10},{10,12},{12,14},{14,16},{16,18},{18... | collective-permute-start | bytes 1572872 | tf_op jit(solution)/shard_map/ppermute | solution.py:12
  128.2 0.8 copy-start.5
  128.2 11.3 %collective-permute-start.2 = (bf16[4,128,512]{2,1,0:T(8,128)(2,1)S(1)}, bf16[4,128,512]{2,1,0:T(8,128)(2,1)S(1)}, u32[]{:S(2)}, u32[]{:S(2)}) collective-permute-start(bf16[4,128,512]{2,1,0:T(8,128)(2,1)S(1)} %collective-permute-done.1), channel_id=1, source_target_pairs={{0,2},{2,4},{4,6},{6,8},{8,10},{10,12},{12,14},{14,16},{16,18},{18... | collective-permute-start | bytes 1572872 | tf_op jit(solution)/shard_map/ppermute | solution.py:12
  139.5 11.3 %collective-permute-start.3 = (bf16[4,128,512]{2,1,0:T(8,128)(2,1)S(1)}, bf16[4,128,512]{2,1,0:T(8,128)(2,1)S(1)}, u32[]{:S(2)}, u32[]{:S(2)}) collective-permute-start(bf16[4,128,512]{2,1,0:T(8,128)(2,1)S(1)} %collective-permute-done.2), channel_id=1, source_target_pairs={{0,2},{2,4},{4,6},{6,8},{8,10},{10,12},{12,14},{14,16},{16,18},{18... | collective-permute-start | bytes 1572872 | tf_op jit(solution)/shard_map/ppermute | solution.py:12
  150.8 0.8 copy-start.4
  150.8 11.3 %collective-permute-start.4 = (bf16[4,128,512]{2,1,0:T(8,128)(2,1)S(1)}, bf16[4,128,512]{2,1,0:T(8,128)(2,1)S(1)}, u32[]{:S(2)}, u32[]{:S(2)}) collective-permute-start(bf16[4,128,512]{2,1,0:T(8,128)(2,1)S(1)} %collective-permute-done.3), channel_id=1, source_target_pairs={{0,2},{2,4},{4,6},{6,8},{8,10},{10,12},{12,14},{14,16},{16,18},{18... | collective-permute-start | bytes 1572872 | tf_op jit(solution)/shard_map/ppermute | solution.py:12
  162.1 11.3 %collective-permute-start.5 = (bf16[4,128,512]{2,1,0:T(8,128)(2,1)S(1)}, bf16[4,128,512]{2,1,0:T(8,128)(2,1)S(1)}, u32[]{:S(2)}, u32[]{:S(2)}) collective-permute-start(bf16[4,128,512]{2,1,0:T(8,128)(2,1)S(1)} %collective-permute-done.4), channel_id=1, source_target_pairs={{0,2},{2,4},{4,6},{6,8},{8,10},{10,12},{12,14},{14,16},{16,18},{18... | collective-permute-start | bytes 1572872 | tf_op jit(solution)/shard_map/ppermute | solution.py:12
  173.4 11.3 %copy-start.3 = (bf16[4,128,512]{2,1,0:T(8,128)(2,1)}, bf16[4,128,512]{2,1,0:T(8,128)(2,1)S(1)}, u32[]{:S(2)}) copy-start(bf16[4,128,512]{2,1,0:T(8,128)(2,1)S(1)} %collective-permute-done.5) | copy-start | bytes 1572868
  173.4 11.3 %collective-permute-start.6 = (bf16[4,128,512]{2,1,0:T(8,128)(2,1)S(1)}, bf16[4,128,512]{2,1,0:T(8,128)(2,1)S(1)}, u32[]{:S(2)}, u32[]{:S(2)}) collective-permute-start(bf16[4,128,512]{2,1,0:T(8,128)(2,1)S(1)} %collective-permute-done.5), channel_id=1, source_target_pairs={{0,2},{2,4},{4,6},{6,8},{8,10},{10,12},{12,14},{14,16},{16,18},{18... | collective-permute-start | bytes 1572872 | tf_op jit(solution)/shard_map/ppermute | solution.py:12
  184.8 11.4 %collective-permute-start.7 = (bf16[4,128,512]{2,1,0:T(8,128)(2,1)S(1)}, bf16[4,128,512]{2,1,0:T(8,128)(2,1)}, u32[]{:S(2)}, u32[]{:S(2)}) collective-permute-start(bf16[4,128,512]{2,1,0:T(8,128)(2,1)S(1)} %collective-permute-done.6), channel_id=1, source_target_pairs={{0,2},{2,4},{4,6},{6,8},{8,10},{10,12},{12,14},{14,16},{16,18},{18... | collective-permute-start | bytes 1572872 | tf_op jit(solution)/shard_map/ppermute | solution.py:12
  196.2 11.5 %collective-permute-start.8 = (bf16[4,128,512]{2,1,0:T(8,128)(2,1)}, bf16[4,128,512]{2,1,0:T(8,128)(2,1)S(1)}, u32[]{:S(2)}, u32[]{:S(2)}) collective-permute-start(bf16[4,128,512]{2,1,0:T(8,128)(2,1)} %collective-permute-done.7), channel_id=1, source_target_pairs={{0,2},{2,4},{4,6},{6,8},{8,10},{10,12},{12,14},{14,16},{16,18},{18... | collective-permute-start | bytes 1572872 | tf_op jit(solution)/shard_map/ppermute | solution.py:12
  200.4 81.5 %copy-start.6 = (f32[16,2]{0,1:T(2,128)S(1)}, f32[16,2]{0,1:T(2,128)}, u32[]{:S(2)}) copy-start(f32[16,2]{0,1:T(2,128)} %param.8) | copy-start | bytes 388
  207.7 11.3 %collective-permute-start.9 = (bf16[4,128,512]{2,1,0:T(8,128)(2,1)S(1)}, bf16[4,128,512]{2,1,0:T(8,128)(2,1)S(1)}, u32[]{:S(2)}, u32[]{:S(2)}) collective-permute-start(bf16[4,128,512]{2,1,0:T(8,128)(2,1)S(1)} %collective-permute-done.8), channel_id=1, source_target_pairs={{0,2},{2,4},{4,6},{6,8},{8,10},{10,12},{12,14},{14,16},{16,18},{18... | collective-permute-start | bytes 1572872 | tf_op jit(solution)/shard_map/ppermute | solution.py:12
  207.7 99.1 %copy-start.1 = (bf16[16,3072]{1,0:T(8,128)(2,1)S(1)}, bf16[16,3072]{1,0:T(8,128)(2,1)}, u32[]{:S(2)}) copy-start(bf16[16,3072]{1,0:T(8,128)(2,1)} %param.6) | copy-start | bytes 294916
  219.0 11.3 %collective-permute-start.10 = (bf16[4,128,512]{2,1,0:T(8,128)(2,1)S(1)}, bf16[4,128,512]{2,1,0:T(8,128)(2,1)S(1)}, u32[]{:S(2)}, u32[]{:S(2)}) collective-permute-start(bf16[4,128,512]{2,1,0:T(8,128)(2,1)S(1)} %collective-permute-done.9), channel_id=1, source_target_pairs={{0,2},{2,4},{4,6},{6,8},{8,10},{10,12},{12,14},{14,16},{16,18},{18... | collective-permute-start | bytes 1572872 | tf_op jit(solution)/shard_map/ppermute | solution.py:12
  230.3 11.3 %collective-permute-start.11 = (bf16[4,128,512]{2,1,0:T(8,128)(2,1)S(1)}, bf16[4,128,512]{2,1,0:T(8,128)(2,1)S(1)}, u32[]{:S(2)}, u32[]{:S(2)}) collective-permute-start(bf16[4,128,512]{2,1,0:T(8,128)(2,1)S(1)} %collective-permute-done.10), channel_id=1, source_target_pairs={{0,2},{2,4},{4,6},{6,8},{8,10},{10,12},{12,14},{14,16},{16,18},{18... | collective-permute-start | bytes 1572872 | tf_op jit(solution)/shard_map/ppermute | solution.py:12
  241.6 11.3 %collective-permute-start.12 = (bf16[4,128,512]{2,1,0:T(8,128)(2,1)S(1)}, bf16[4,128,512]{2,1,0:T(8,128)(2,1)S(1)}, u32[]{:S(2)}, u32[]{:S(2)}) collective-permute-start(bf16[4,128,512]{2,1,0:T(8,128)(2,1)S(1)} %collective-permute-done.11), channel_id=1, source_target_pairs={{0,2},{2,4},{4,6},{6,8},{8,10},{10,12},{12,14},{14,16},{16,18},{18... | collective-permute-start | bytes 1572872 | tf_op jit(solution)/shard_map/ppermute | solution.py:12
  252.9 11.3 %collective-permute-start.13 = (bf16[4,128,512]{2,1,0:T(8,128)(2,1)S(1)}, bf16[4,128,512]{2,1,0:T(8,128)(2,1)S(1)}, u32[]{:S(2)}, u32[]{:S(2)}) collective-permute-start(bf16[4,128,512]{2,1,0:T(8,128)(2,1)S(1)} %collective-permute-done.12), channel_id=1, source_target_pairs={{0,2},{2,4},{4,6},{6,8},{8,10},{10,12},{12,14},{14,16},{16,18},{18... | collective-permute-start | bytes 1572872 | tf_op jit(solution)/shard_map/ppermute | solution.py:12
  264.2 11.3 %collective-permute-start.14 = (bf16[4,128,512]{2,1,0:T(8,128)(2,1)S(1)}, bf16[4,128,512]{2,1,0:T(8,128)(2,1)S(1)}, u32[]{:S(2)}, u32[]{:S(2)}) collective-permute-start(bf16[4,128,512]{2,1,0:T(8,128)(2,1)S(1)} %collective-permute-done.13), channel_id=1, source_target_pairs={{0,2},{2,4},{4,6},{6,8},{8,10},{10,12},{12,14},{14,16},{16,18},{18... | collective-permute-start | bytes 1572872 | tf_op jit(solution)/shard_map/ppermute | solution.py:12
  278.3 15.7 %all-to-all-start.1 = ((bf16[4,16,8,384]{3,2,0,1:T(8,128)(2,1)}), bf16[4,16,8,384]{3,2,0,1:T(8,128)(2,1)S(1)}, u32[]{:S(2)}, u32[]{:S(2)}) async-start(bf16[4,16,8,384]{3,2,0,1:T(8,128)(2,1)} %copy.22), calls=%async_computation.1 | async-start | bytes 786432 | tf_op jit(solution)/shard_map/all_to_all | solution.py:66
  295.0 10.6 %all-to-all-start.2 = ((bf16[4,8,2,3072]{3,1,0,2:T(8,128)(2,1)}), bf16[4,8,2,3072]{3,1,0,2:T(8,128)(2,1)S(1)}, u32[]{:S(2)}, u32[]{:S(2)}) async-start(bf16[4,8,2,3072]{3,1,0,2:T(8,128)(2,1)} %copy.24), calls=%async_computation.2 | async-start | bytes 786432 | tf_op jit(solution)/shard_map/all_to_all | solution.py:70
Sparse Core Ops, SparseCore 0:
  20.0 61.8 all-gather.1
